TPU v7x, 32 devices: a whole 2x2x4 slice. The times are simulated.
32 devices in a mesh: frame: 4 (over x, core), seq: 8 (over z, y).
Axes of the slice: x: 2, y: 2, z: 4, core: 2. Of those that a mesh axis runs over, the one named last changes fastest.
Arguments:
- vit_states: bfloat16 [64, 256, 1280], P(('frame', 'seq')), may hold values from -6 to 6
- frame_slot: int32 [32], replicated, may hold values from 0 to 63, as said below
- patch_count: int32 [32], replicated, may hold values from 208 to 256, as said below
- vis_start: int32 [32], replicated, may hold values from 0 to 4095, as said below
- text_embed: bfloat16 [128, 32, 4096], P(None, ('frame', 'seq')), may hold values from -6 to 6
- vit_ln_gain: float32 [1280], replicated, may hold values from 0.25 to 1.75
- vit_ln_bias: float32 [1280], replicated, may hold values from -1.5 to 1.5
- vit_qkv_w: bfloat16 [1280, 3840], P('seq'), may hold values from -0.15625 to 0.15625
- vit_qkv_b: float32 [3840], replicated, may hold values from -1.5 to 1.5
- vit_out_w: bfloat16 [1280, 1280], P('seq'), may hold values from -0.15625 to 0.15625
- vit_out_b: float32 [1280], replicated, may hold values from -1.5 to 1.5
- proj_w: bfloat16 [1280, 4096], replicated, may hold values from -0.15625 to 0.15625
- proj_b: float32 [4096], replicated, may hold values from -1.5 to 1.5
- attn_gain: float32 [4096], replicated, may hold values from 0.25 to 1.75
- wq: bfloat16 [4096, 2048], P(None, 'frame'), may hold values from -0.09375 to 0.09375
- wk: bfloat16 [4096, 1024], P(None, 'frame'), may hold values from -0.09375 to 0.09375
- wv: bfloat16 [4096, 1024], P(None, 'frame'), may hold values from -0.09375 to 0.09375
- wo: bfloat16 [2048, 4096], P('frame'), may hold values from -0.125 to 0.125
Outputs:
- mixed: bfloat16 [128, 32, 4096], P(None, ('frame', 'seq'))
Inputs may be any that keep to these rules, and one draw needn't show every extreme that they name: Frame t sits in slot frame_slot[t]; slot k of the device with index d (axes frame then seq) is d * 2 + k; no slot holds two frames. The two devices with frame indices 2i and 2i+1 and the same seq index hold exactly two frames between them; some device holds 2 frames. `patch_count`: A multiple of 4; some frame has 256 patches. Frame t's patch_count[t] / 4 visual positions start at vis_start[t] and lie within positions t * 128 to (t + 1) * 128 - 1.
All inputs are finite; a program needn't handle non-finite values.
Results may differ from a plain program's by a relative error of at most 0.015.
Values may be sent and summed in bfloat16 or wider, within the bound.
A program may use at most 128 MiB of HBM per device.

v0:
```python
import math
import jax
import jax.numpy as jnp
from jax import lax
from jax.sharding import PartitionSpec as P

VHEADS = 16
HEAD_WIDTH = 128
rope_theta = 500000.0
vit_epsilon = 1e-06
norm_epsilon = 1e-05
masked_score = -1e30


def partner_2(value, axis, stride):
    mask = 2**stride
    pairs = [(source, source ^ mask) for source in range(lax.axis_size(axis))]
    return lax.ppermute(value, axis, pairs)


def apply_rotary(values, rotary_angles):
    half_width = values.shape[-1] // 2
    first_half = values[..., :half_width]
    second_half = values[..., half_width:]
    cosine = jnp.cos(rotary_angles)
    sine_part = jnp.sin(rotary_angles)
    return jnp.concatenate(
        [
            first_half * cosine - second_half * sine_part,
            second_half * cosine + first_half * sine_part,
        ],
        axis=-1,
    )


def rope_angles(positions, head_size):
    exponents = jnp.arange(0, head_size, 2).astype(jnp.float32) / head_size
    inverse = jnp.power(jnp.float32(rope_theta), -exponents)
    return positions.astype(jnp.float32)[:, None] * inverse[None, :]


def add_columns(left, shard_piece):
    return jnp.dot(left, shard_piece, preferred_element_type=jnp.float32)


def per_device(
    vit_states,
    frame_slot,
    patch_count,
    vis_start,
    text_embed,
    vit_ln_gain,
    vit_ln_bias,
    vit_qkv_w,
    vit_qkv_b,
    vit_out_w,
    vit_out_b,
    proj_w,
    proj_b,
    attn_gain,
    wq,
    wk,
    wv,
    wo,
):
    frames_n = lax.axis_size("frame")
    seqs_n = lax.axis_size("seq")
    devices_n = frames_n * seqs_n
    my_frame = lax.axis_index("frame")
    my_seq = lax.axis_index("seq")
    my_device = my_frame * seqs_n + my_seq
    slots_held = vit_states.shape[0]
    frame_max = vit_states.shape[1]
    width_vit = vit_states.shape[2]
    vis_max = frame_max // 4
    own_rows = text_embed.shape[0]
    laps = (vis_max + devices_n - 1) // devices_n
    frame_ids = jnp.arange(frame_slot.shape[0])
    holder = frame_slot // slots_held
    holder_frame = holder // seqs_n
    pair_low = (holder_frame - holder_frame % 2) * seqs_n + holder % seqs_n
    pair_order = holder_frame % 2 * slots_held + frame_slot % slots_held
    same_pair = pair_low[:, None] == pair_low[None, :]
    earlier = pair_order[None, :] < pair_order[:, None]
    pair_rank = jnp.sum((same_pair & earlier).astype(jnp.int32), axis=1)
    partner = partner_2(vit_states, "frame", 0)
    low_side = my_frame % 2 == 0
    four_slots = jnp.where(
        low_side,
        jnp.concatenate([vit_states, partner], 0),
        jnp.concatenate([partner, vit_states], 0),
    )
    my_low = (my_frame - my_frame % 2) * seqs_n + my_seq
    picked = (pair_low == my_low) & (pair_rank == my_frame % 2)
    my_frame_id = jnp.sum(jnp.where(picked, frame_ids, 0))
    my_order = jnp.sum(jnp.where(picked, pair_order, 0))
    states = lax.dynamic_slice_in_dim(four_slots, my_order, 1, 0)
    slots_n = 1
    slot_frames = jnp.reshape(my_frame_id, (1,))
    slot_live = jnp.ones((1,), jnp.bool_)
    source_device = pair_low + pair_rank * seqs_n
    slot_count = jnp.where(slot_live, patch_count[slot_frames], frame_max)
    slot_start = vis_start[slot_frames]
    patch_rows = states.reshape(slots_n * frame_max, width_vit)
    rows_wide = patch_rows.astype(jnp.float32)
    average = jnp.mean(rows_wide, axis=1, keepdims=True)
    centred = rows_wide - average
    spread = jnp.mean(centred * centred, axis=1, keepdims=True)
    normed_states = (centred * lax.rsqrt(spread + vit_epsilon) * vit_ln_gain + vit_ln_bias).astype(
        jnp.bfloat16
    )
    projected_vit = add_columns(normed_states, lax.all_gather(vit_qkv_w, "seq", axis=0, tiled=True))
    projected_vit = (projected_vit + vit_qkv_b).astype(jnp.bfloat16)
    head_size = width_vit // VHEADS
    shaped = projected_vit.reshape(slots_n, frame_max, 3, VHEADS, head_size)
    scores = jnp.einsum(
        "sqhd,skhd->shqk", shaped[:, :, 0], shaped[:, :, 1], preferred_element_type=jnp.float32
    ) / math.sqrt(head_size)
    key_live = jnp.arange(frame_max)[None, :] < slot_count[:, None]
    scores = jnp.where(key_live[:, None, None, :], scores, masked_score)
    highest = jnp.max(scores, axis=-1, keepdims=True)
    weights = jnp.exp(scores - highest)
    probabilities = (weights / jnp.sum(weights, axis=-1, keepdims=True)).astype(jnp.bfloat16)
    context_vit = jnp.einsum(
        "shqk,skhd->sqhd", probabilities, shaped[:, :, 2], preferred_element_type=jnp.float32
    ).astype(jnp.bfloat16)
    context_vit = context_vit.reshape(patch_rows.shape[0], width_vit)
    attended = add_columns(context_vit, lax.all_gather(vit_out_w, "seq", axis=0, tiled=True))
    hidden = (rows_wide + attended + vit_out_b).astype(jnp.bfloat16)
    pooled = jnp.mean(
        hidden.astype(jnp.float32).reshape(slots_n, vis_max, 4, width_vit), axis=2
    ).astype(jnp.bfloat16)
    owners = jnp.arange(devices_n)
    lap_ids = jnp.arange(laps)
    distance = jnp.mod(owners[:, None] - slot_start[None, :], devices_n)
    token_ids = distance[:, :, None] + lap_ids[None, None, :] * devices_n
    sent_live = (token_ids < (slot_count // 4)[None, :, None]) & slot_live[None, :, None]
    token_clip = jnp.minimum(token_ids, vis_max - 1)
    slot_ids = jnp.arange(slots_n)[None, :, None]
    outgoing = jnp.where(
        sent_live[..., None], pooled[slot_ids, token_clip], jnp.zeros((), jnp.bfloat16)
    )
    arrived = lax.all_to_all(outgoing, ("frame", "seq"), split_axis=0, concat_axis=0, tiled=True)
    local_ids = jnp.arange(own_rows)
    positions = local_ids * devices_n + my_device
    token_frame = positions // own_rows
    within = positions - vis_start[token_frame]
    is_visual = (within >= 0) & (within < patch_count[token_frame] // 4)
    within_clip = jnp.clip(within, 0, vis_max - 1)
    flat_index = source_device[token_frame] * slots_n * laps + within_clip // devices_n
    table = arrived.reshape(devices_n * slots_n * laps, arrived.shape[-1])
    fetched = table[flat_index]
    fetched = (jnp.dot(fetched, proj_w, preferred_element_type=jnp.float32) + proj_b).astype(
        jnp.bfloat16
    )
    text_rows = text_embed.reshape(own_rows, text_embed.shape[-1])
    merged = jnp.where(is_visual[:, None], fetched, text_rows)
    merged_wide = merged.astype(jnp.float32)
    normed_tok = (
        merged_wide
        * lax.rsqrt(jnp.mean(merged_wide * merged_wide, axis=1, keepdims=True) + norm_epsilon)
        * attn_gain
    ).astype(jnp.bfloat16)
    shard_piece = lax.all_gather(normed_tok, "frame", axis=0, tiled=True)
    projected = jnp.concatenate(
        [
            jnp.dot(shard_piece, wq, preferred_element_type=jnp.float32),
            jnp.dot(shard_piece, wk, preferred_element_type=jnp.float32),
            jnp.dot(shard_piece, wv, preferred_element_type=jnp.float32),
        ],
        axis=1,
    )
    query_width = wq.shape[1]
    kv_width = wk.shape[1]
    group_rows = projected.shape[0]
    kv_heads = kv_width // HEAD_WIDTH
    query_heads = query_width // HEAD_WIDTH
    row_ids = jnp.arange(group_rows)
    group_positions = row_ids % own_rows * devices_n + row_ids // own_rows * seqs_n + my_seq
    rotary_angles = rope_angles(group_positions, HEAD_WIDTH)[:, None, :]
    query_matrix = apply_rotary(
        projected[:, :query_width].reshape(group_rows, query_heads, HEAD_WIDTH), rotary_angles
    ).astype(jnp.bfloat16)
    keys_own = apply_rotary(
        projected[:, query_width : query_width + kv_width].reshape(
            group_rows, kv_heads, HEAD_WIDTH
        ),
        rotary_angles,
    ).astype(jnp.bfloat16)
    values_own = (
        projected[:, query_width + kv_width :]
        .astype(jnp.bfloat16)
        .reshape(group_rows, kv_heads, HEAD_WIDTH)
    )
    grouped_rows = query_matrix.reshape(group_rows, kv_heads, query_heads // kv_heads, HEAD_WIDTH)
    group_size = query_heads // kv_heads
    start_state = (
        jnp.full((kv_heads, group_size, group_rows), masked_score, jnp.float32),
        jnp.zeros((kv_heads, group_size, group_rows), jnp.float32),
        jnp.zeros((kv_heads, group_size, group_rows, HEAD_WIDTH), jnp.float32),
    )
    carry = start_state
    key_piece = lax.all_gather(keys_own, "seq", axis=0, tiled=True)
    value_piece = lax.all_gather(values_own, "seq", axis=0, tiled=True)
    piece_rows = key_piece.shape[0]
    inner_rows = math.gcd(piece_rows, 1024)
    steps_n = piece_rows // inner_rows
    key_blocks = key_piece.reshape(steps_n, inner_rows, kv_heads, HEAD_WIDTH)
    value_blocks = value_piece.reshape(steps_n, inner_rows, kv_heads, HEAD_WIDTH)
    block_offsets = inner_rows * jnp.arange(steps_n)

    def visit(running, operands):
        running_max, denominator, weighted = running
        key_block, value_block, block_offset = operands
        gathered_ids = block_offset + jnp.arange(inner_rows)
        seq_of = gathered_ids // group_rows
        inner_ids = gathered_ids % group_rows
        key_positions = inner_ids % own_rows * devices_n + inner_ids // own_rows * seqs_n + seq_of
        block_scores = jnp.einsum(
            "qkgd,nkd->kgqn", grouped_rows, key_block, preferred_element_type=jnp.float32
        ) / math.sqrt(HEAD_WIDTH)
        allowed = key_positions[None, :] <= group_positions[:, None]
        block_scores = jnp.where(allowed[None, None], block_scores, masked_score)
        new_max = jnp.maximum(running_max, jnp.max(block_scores, axis=-1))
        expd = jnp.where(allowed[None, None], jnp.exp(block_scores - new_max[..., None]), 0.0)
        rescale = jnp.exp(running_max - new_max)
        denominator = denominator * rescale + jnp.sum(expd, axis=-1)
        weighted = weighted * rescale[..., None] + jnp.einsum(
            "kgqn,nkd->kgqd",
            expd.astype(jnp.bfloat16),
            value_block,
            preferred_element_type=jnp.float32,
        )
        return ((new_max, denominator, weighted), None)

    carry, unused = lax.scan(visit, carry, (key_blocks, value_blocks, block_offsets))
    final_max, denominator, weighted = carry
    context_tok = (weighted / denominator[..., None]).astype(jnp.bfloat16)
    context_tok = jnp.transpose(context_tok, (2, 0, 1, 3)).reshape(group_rows, query_width)
    summed = lax.psum_scatter(
        jnp.dot(context_tok, wo, preferred_element_type=jnp.float32).astype(jnp.bfloat16),
        "frame",
        scatter_dimension=0,
        tiled=True,
    )
    return summed.reshape(own_rows, 1, wo.shape[1])


def solution(mesh):
    return jax.shard_map(
        per_device,
        mesh=mesh,
        in_specs=(
            P(("frame", "seq"), None, None),
            P(),
            P(),
            P(),
            P(None, ("frame", "seq"), None),
            P(),
            P(),
            P("seq", None),
            P(),
            P("seq", None),
            P(),
            P(),
            P(),
            P(),
            P(None, "frame"),
            P(None, "frame"),
            P(None, "frame"),
            P("frame", None),
        ),
        out_specs=P(None, ("frame", "seq"), None),
        check_vma=False,
    )
```

profile of v0, /device:TPU:0, one launch (start us, length us, event | category | flops | bytes accessed | tf_op | source)
XLA Modules:
  0.0 512.4 jit_solution(6202785359800764585)
XLA Ops:
  26.0 1.9 convert_reduce_fusion
  28.2 126.3 %all-gather.6.cloned.1.call-done = bf16[1280,3840]{1,0:T(8,128)(2,1)} async-done(((bf16[160,3840]{1,0:T(8,128)(2,1)}), bf16[1280,3840]{1,0:T(8,128)(2,1)}) %all-gather.6.cloned.1.call-update) | async-done | bytes 9830416 | tf_op jit(solution)/shard_map/all_gather | solution.py:112
  154.5 7.9 %fusion.48 = bf16[256,3840]{1,0:T(8,128)(2,1)} fusion(bf16[1280,3840]{1,0:T(8,128)(2,1)} %all-gather.6.cloned.1.call-done, f32[3840]{0:T(1024)S(1)} %copy-done.5, bf16[1,256,1280]{2,1,0:T(8,128)(2,1)S(1)} %get-tuple-element.277, f32[1280]{0:T(1024)S(1)} %copy-done.6, f32[1280]{0:T(1024)S(1)} %copy-done.7, f32[256]{0:T(256)S(1)} %add_rsqrt_fusion, ...), kind=kOutput, calls=%fused_computation.75 | convolution fusion | flops 2520514560 | bytes 12479488 | tf_op jit(solution)/shard_map/dot_general | solution.py:43
  162.4 4.0 copy.73
  166.4 2.0 fusion.72
  168.5 1.7 fusion.102
  171.8 44.6 %all-gather.8.cloned.1.call-done = bf16[1280,1280]{1,0:T(8,128)(2,1)} async-done(((bf16[160,1280]{1,0:T(8,128)(2,1)}), bf16[1280,1280]{1,0:T(8,128)(2,1)}) %all-gather.8.cloned.1.call-update) | async-done | bytes 3276816 | tf_op jit(solution)/shard_map/all_gather | solution.py:128
  216.4 4.0 fusion.55
  226.7 3.3 all-to-all-start
  230.3 7.7 %all-to-all-done = bf16[32,1,2,1280]{3,2,1,0:T(2,128)(2,1)S(1)} async-done(((bf16[32,1,2,1280]{3,2,1,0:T(2,128)(2,1)}), bf16[32,1,2,1280]{3,2,1,0:T(2,128)(2,1)S(1)}, u32[]{:S(2)}, u32[]{:S(2)}) %all-to-all-start) | async-done | bytes 163872 | tf_op jit(solution)/shard_map/all_to_all | solution.py:143
  239.0 6.3 %multiply_reduce_fusion = (f32[128]{0:T(128)S(1)}, f32[128,4096]{1,0:T(8,128)S(1)}) fusion(bf16[128,1,4096]{2,0,1:T(8,128)(2,1)} %param.24, f32[4096]{0:T(1024)S(1)} %copy-done.3, bf16[128,1280]{1,0:T(8,128)(2,1)S(1)} %gather_fusion.4, bf16[1280,4096]{1,0:T(8,128)(2,1)} %param.31, pred[128]{0:T(512)(128)(4,1)S(1)} %compare_and_fusion.1), kind=kOutput, calls=%fused_computation.93 | convolution fusion | flops 1345322880 | bytes 13976192 | tf_op jit(solution)/shard_map/dot_general | solution.py:153
  247.5 32.0 %all-gather.10.cloned.1.call-done = bf16[512,4096]{1,0:T(8,128)(2,1)} async-done(((bf16[128,4096]{1,0:T(8,128)(2,1)}), bf16[512,4096]{1,0:T(8,128)(2,1)}) %all-gather.10.cloned.1.call-update) | async-done | bytes 4194320 | tf_op jit(solution)/shard_map/all_gather | solution.py:164
  279.5 3.5 fusion.103
  284.5 4.2 convolution_convert_fusion.1
  289.6 6.0 %fusion.104 = f32[512,512]{0,1:T(8,128)S(1)} fusion(bf16[512,4096]{1,0:T(8,128)(2,1)} %all-gather.10.cloned.1.call-done, bf16[4096,512]{1,0:T(8,128)(2,1)} %param.34), kind=kOutput, calls=%fused_computation.213 | convolution fusion | flops 2147483648 | bytes 9437184 | tf_op jit(solution)/shard_map/dot_general | solution.py:167
  296.7 37.0 %all-gather.12.cloned.1.call-done = bf16[4096,2,128]{2,0,1:T(8,128)(2,1)} async-done(((bf16[512,2,128]{2,0,1:T(8,128)(2,1)}), bf16[4096,2,128]{2,0,1:T(8,128)(2,1)}) %all-gather.12.cloned.1.call-update) | async-done | bytes 2097168 | tf_op jit(solution)/shard_map/all_gather | solution.py:203
  333.7 49.7 %all-gather.14.cloned.1.call-done = bf16[4096,2,128]{2,0,1:T(8,128)(2,1)} async-done(((bf16[512,2,128]{2,0,1:T(8,128)(2,1)}), bf16[4096,2,128]{2,0,1:T(8,128)(2,1)}) %all-gather.14.cloned.1.call-update) | async-done | bytes 2097168 | tf_op jit(solution)/shard_map/all_gather | solution.py:204
  383.3 71.8 %while.20 = (s32[]{:T(128)}, f32[2,2,512]{2,1,0:T(2,128)S(1)}, f32[2,2,512]{2,1,0:T(2,128)S(1)}, f32[2,2,512,128]{3,2,1,0:T(8,128)S(1)}, s32[4]{0:T(128)S(1)}, /...) while((s32[]{:T(128)}, f32[2,2,512]{2,1,0:T(2,128)S(1)}, ...), condition=%wide.region_12.13_spmd.clone, body=%wide.region_9.12_spmd.clone.sunk | while | flops 1102377984 | bytes 64631976 | solution.py:236
  385.0 5.9 %fusion.134 = (f32[2,2,512]{2,1,0:T(2,128)S(1)}, f32[2,1024,512,2]{2,1,3,0:T(8,128)}) fusion(pred[512,1024]{0,1:T(8,128)(4,1)S(1)} %broadcast_compare_fusion.2, bf16[512,2,2,128]{3,0,2,1:T(8,128)(2,1)S(1)} %get-tuple-element.390, bf16[4,1024,2,128]{3,1,0,2:T(8,128)(2,1)} %get-tuple-element.389, s32[]{:T(128)} %get-tuple-element.373), kind=kOutput, calls=%fused_computation.8.clone.1 | convolution fusion | flops 543160320 | bytes 9970176 | tf_op jit(solution)/shard_map/while/body/eval_jaxpr/qkgd,nkd->kgqn/dot_general | solution.py:219
  390.8 4.6 fusion.136
  396.7 4.6 fusion.138
  402.9 5.9 %fusion.134 = (f32[2,2,512]{2,1,0:T(2,128)S(1)}, f32[2,1024,512,2]{2,1,3,0:T(8,128)}) fusion(pred[512,1024]{0,1:T(8,128)(4,1)S(1)} %broadcast_compare_fusion.2, bf16[512,2,2,128]{3,0,2,1:T(8,128)(2,1)S(1)} %get-tuple-element.390, bf16[4,1024,2,128]{3,1,0,2:T(8,128)(2,1)} %get-tuple-element.389, s32[]{:T(128)} %get-tuple-element.373), kind=kOutput, calls=%fused_computation.8.clone.1 | convolution fusion | flops 543160320 | bytes 9970176 | tf_op jit(solution)/shard_map/while/body/eval_jaxpr/qkgd,nkd->kgqn/dot_general | solution.py:219
  408.8 4.6 fusion.136
  414.6 4.6 fusion.138
  420.9 5.9 %fusion.134 = (f32[2,2,512]{2,1,0:T(2,128)S(1)}, f32[2,1024,512,2]{2,1,3,0:T(8,128)}) fusion(pred[512,1024]{0,1:T(8,128)(4,1)S(1)} %broadcast_compare_fusion.2, bf16[512,2,2,128]{3,0,2,1:T(8,128)(2,1)S(1)} %get-tuple-element.390, bf16[4,1024,2,128]{3,1,0,2:T(8,128)(2,1)} %get-tuple-element.389, s32[]{:T(128)} %get-tuple-element.373), kind=kOutput, calls=%fused_computation.8.clone.1 | convolution fusion | flops 543160320 | bytes 9970176 | tf_op jit(solution)/shard_map/while/body/eval_jaxpr/qkgd,nkd->kgqn/dot_general | solution.py:219
  426.7 4.6 fusion.136
  432.6 4.6 fusion.138
  438.8 5.9 %fusion.134 = (f32[2,2,512]{2,1,0:T(2,128)S(1)}, f32[2,1024,512,2]{2,1,3,0:T(8,128)}) fusion(pred[512,1024]{0,1:T(8,128)(4,1)S(1)} %broadcast_compare_fusion.2, bf16[512,2,2,128]{3,0,2,1:T(8,128)(2,1)S(1)} %get-tuple-element.390, bf16[4,1024,2,128]{3,1,0,2:T(8,128)(2,1)} %get-tuple-element.389, s32[]{:T(128)} %get-tuple-element.373), kind=kOutput, calls=%fused_computation.8.clone.1 | convolution fusion | flops 543160320 | bytes 9970176 | tf_op jit(solution)/shard_map/while/body/eval_jaxpr/qkgd,nkd->kgqn/dot_general | solution.py:219
  444.7 4.6 fusion.136
  450.5 4.6 fusion.138
  455.6 6.6 %convolution_convert_fusion = bf16[512,4096]{1,0:T(8,128)(2,1)} fusion(bf16[512,512]{0,1:T(8,128)(2,1)S(1)} %bitcast.138, bf16[512,4096]{1,0:T(8,128)(2,1)} %param.37), kind=kOutput, calls=%fused_computation.73 | convolution fusion | flops 2149580800 | bytes 8912896 | tf_op jit(solution)/shard_map/dot_general | solution.py:241
  462.3 43.3 %reduce-scatter.2.cloned.1.call-done = bf16[128,4096]{1,0:T(8,128)(2,1)} async-done(((bf16[512,4096]{1,0:T(8,128)(2,1)}), bf16[128,4096]{1,0:T(8,128)(2,1)}) %reduce-scatter.2.cloned.1.call-update) | async-done | bytes 1048592 | tf_op jit(solution)/shard_map/reduce_scatter | solution.py:240
  (127 shorter events, 39.2 us)
Async XLA Ops:
  6.5 272.9 %copy-start = (bf16[4096,256]{1,0:T(8,128)(2,1)S(1)}, bf16[4096,256]{1,0:T(8,128)(2,1)}, u32[]{:S(2)}) copy-start(bf16[4096,256]{1,0:T(8,128)(2,1)} %param.35) | copy-start | bytes 6291460
  6.5 148.0 %copy-start.7 = (f32[1280]{0:T(1024)S(1)}, f32[1280]{0:T(1024)}, u32[]{:S(2)}) copy-start(f32[1280]{0:T(1024)} %param.25) | copy-start | bytes 15364
  6.5 148.0 %copy-start.6 = (f32[1280]{0:T(1024)S(1)}, f32[1280]{0:T(1024)}, u32[]{:S(2)}) copy-start(f32[1280]{0:T(1024)} %param.26) | copy-start | bytes 15364
  6.5 148.0 %copy-start.5 = (f32[3840]{0:T(1024)S(1)}, f32[3840]{0:T(1024)}, u32[]{:S(2)}) copy-start(f32[3840]{0:T(1024)} %param.28) | copy-start | bytes 46084
  6.5 148.0 %all-gather.6.cloned.1.call-start = ((), (), s32[]{:S(2)}) async-start(), calls=%async_computation.2 | async-start | bytes 11059200 | tf_op jit(solution)/shard_map/all_gather | solution.py:112
  7.3 209.1 %all-gather.8.cloned.1.call-start = ((), (), s32[]{:S(2)}) async-start(), calls=%async_computation.3 | async-start | bytes 3686400 | tf_op jit(solution)/shard_map/all_gather | solution.py:128
  7.3 18.7 %collective-permute-start = (bf16[2,256,1280]{2,1,0:T(8,128)(2,1)}, bf16[2,256,1280]{2,1,0:T(8,128)(2,1)}, u32[]{:S(2)}, u32[]{:S(2)}) collective-permute-start(bf16[2,256,1280]{2,1,0:T(8,128)(2,1)} %param.20), channel_id=1, source_target_pairs={{0,8},{8,0},{16,24},{24,16},{1,9},{9,1},{17,25},{25,17},{2,10},{10... | collective-permute-start | bytes 3932168 | tf_op jit(solution)/shard_map/ppermute | solution.py:18
  170.2 46.2 %copy-start.8 = (f32[1280]{0:T(1024)S(1)}, f32[1280]{0:T(1024)}, u32[]{:S(2)}) copy-start(f32[1280]{0:T(1024)} %param.30) | copy-start | bytes 15364
  222.1 16.9 %copy-start.3 = (f32[4096]{0:T(1024)S(1)}, f32[4096]{0:T(1024)}, u32[]{:S(2)}) copy-start(f32[4096]{0:T(1024)} %param.32) | copy-start | bytes 49156
  226.7 11.3 %all-to-all-start = ((bf16[32,1,2,1280]{3,2,1,0:T(2,128)(2,1)}), bf16[32,1,2,1280]{3,2,1,0:T(2,128)(2,1)S(1)}, u32[]{:S(2)}, u32[]{:S(2)}) async-start(bf16[32,1,2,1280]{3,2,1,0:T(2,128)(2,1)} %broadcast_select_fusion.1), calls=%async_computation | async-start | bytes 327680 | tf_op jit(solution)/shard_map/all_to_all | solution.py:143
  230.0 49.4 %all-gather.10.cloned.1.call-start = ((), (), s32[]{:S(2)}) async-start(), calls=%async_computation.4 | async-start | bytes 5242880 | tf_op jit(solution)/shard_map/all_gather | solution.py:164
  239.0 6.3 %copy-start.4 = (f32[4096]{0:T(1024)S(1)}, f32[4096]{0:T(1024)}, u32[]{:S(2)}) copy-start(f32[4096]{0:T(1024)} %param.33) | copy-start | bytes 49156
  246.6 87.1 %all-gather.12.cloned.1.call-start = ((), (), s32[]{:S(2)}) async-start(), calls=%async_computation.5 | async-start | bytes 2359296 | tf_op jit(solution)/shard_map/all_gather | solution.py:203
  284.4 98.9 %all-gather.14.cloned.1.call-start = ((), (), s32[]{:S(2)}) async-start(), calls=%async_computation.6 | async-start | bytes 2359296 | tf_op jit(solution)/shard_map/all_gather | solution.py:204
  289.5 216.0 %reduce-scatter.2.cloned.1.call-start = ((), (), s32[]{:S(2)}) async-start(), calls=%async_computation.7 | async-start | bytes 5242880 | tf_op jit(solution)/shard_map/reduce_scatter | solution.py:240
  390.8 5.8 %copy-start.2 = (f32[2,1024,512,2]{2,1,3,0:T(8,128)S(1)}, f32[2,1024,512,2]{2,1,3,0:T(8,128)}, u32[]{:S(2)}) copy-start(f32[2,1024,512,2]{2,1,3,0:T(8,128)} %get-tuple-element.359) | copy-start | bytes 25165828 | tf_op jit(solution)/shard_map/while
  408.8 5.8 %copy-start.2 = (f32[2,1024,512,2]{2,1,3,0:T(8,128)S(1)}, f32[2,1024,512,2]{2,1,3,0:T(8,128)}, u32[]{:S(2)}) copy-start(f32[2,1024,512,2]{2,1,3,0:T(8,128)} %get-tuple-element.359) | copy-start | bytes 25165828 | tf_op jit(solution)/shard_map/while
  426.7 5.8 %copy-start.2 = (f32[2,1024,512,2]{2,1,3,0:T(8,128)S(1)}, f32[2,1024,512,2]{2,1,3,0:T(8,128)}, u32[]{:S(2)}) copy-start(f32[2,1024,512,2]{2,1,3,0:T(8,128)} %get-tuple-element.359) | copy-start | bytes 25165828 | tf_op jit(solution)/shard_map/while
  444.7 5.8 %copy-start.2 = (f32[2,1024,512,2]{2,1,3,0:T(8,128)S(1)}, f32[2,1024,512,2]{2,1,3,0:T(8,128)}, u32[]{:S(2)}) copy-start(f32[2,1024,512,2]{2,1,3,0:T(8,128)} %get-tuple-element.359) | copy-start | bytes 25165828 | tf_op jit(solution)/shard_map/while
  455.6 50.0 %copy-start.1 = (bf16[4096,256]{1,0:T(8,128)(2,1)S(1)}, bf16[4096,256]{1,0:T(8,128)(2,1)}, u32[]{:S(2)}) copy-start(bf16[4096,256]{1,0:T(8,128)(2,1)} %param.35) | copy-start | bytes 6291460
Sparse Core Ops, SparseCore 0:
  9.5 144.9 all-gather.5
  156.7 59.6 all-gather.7
  246.7 32.7 all-gather.9
  284.6 49.0 all-gather.11
  335.7 47.5 all-gather.13
  462.4 43.1 reduce-scatter.1
where the time goes:
time: 513 us; the launch traced here: 512 us
  waiting for transfers between devices  341 us (66%)
  matrix products  83.9 us (16%)
  other arithmetic  37.4 us (7%)
  local copies, waits for them, and re-layouts  24.6 us (5%)
  between operations  20.7 us (4%)
    all_gather x1, waiting for transfers between devices, per_device(): lax.all_gather(vit_qkv_w, 'seq', axis=0, tiled=True)  126 us
    all_gather x1, waiting for transfers between devices, per_device(): value_piece = lax.all_gather(values_own, 'seq', axis=0, tiled=True)  49.7 us
    all_gather x1, waiting for transfers between devices, per_device(): lax.all_gather(vit_out_w, 'seq', axis=0, tiled=True)  44.6 us
    reduce_scatter x1, waiting for transfers between devices, per_device(): lax.psum_scatter(jnp.dot(context_tok, wo, preferred_element_type=jnp.floa...  43.3 us
    all_gather x1, waiting for transfers between devices, per_device(): key_piece = lax.all_gather(keys_own, 'seq', axis=0, tiled=True)  37 us
    all_gather x1, waiting for transfers between devices, per_device(): shard_piece = lax.all_gather(normed_tok, 'frame', axis=0, tiled=True)  32 us
    dot_general x4, matrix products, visit(): jnp.einsum('qkgd,nkd->kgqn', grouped_rows, key_block, preferred_element_t...  23.4 us
    reduce_sum x4, other arithmetic, visit(): denominator = denominator * rescale + jnp.sum(expd, axis=-1)  18.6 us
  transfers between devices with their start and end apart: 8, of which 7 were waited for; matrix products, arithmetic and copies ran while one was open for 8% of the time, Pallas kernels for 0%

commit v1 on v0

--- a/solution.py
+++ b/solution.py
@@ -201,7 +201,14 @@
     )
     carry = start_state
     key_piece = lax.all_gather(keys_own, "seq", axis=0, tiled=True)
-    value_piece = lax.all_gather(values_own, "seq", axis=0, tiled=True)
+    devices = lax.axis_size("seq")
+    right = [(i, (i + 1) % devices) for i in range(devices)]
+    parts = [values_own]
+    for far in range(1, devices):
+        parts = [lax.ppermute(parts[0], "seq", right), *parts]
+    result = jnp.concatenate(parts, axis=0)
+    places = (lax.axis_index("seq") + 1) * parts[-1].shape[0]
+    value_piece = jnp.roll(result, places, axis=0)
     piece_rows = key_piece.shape[0]
     inner_rows = math.gcd(piece_rows, 1024)
     steps_n = piece_rows // inner_rows

time: 513 us -> 508 us (level)
  waiting for transfers between devices: 341 us -> 323 us
  local copies, waits for them, and re-layouts: 24.6 us -> 34.6 us
    ppermute x0 -> x7, waiting for transfers between devices: none -> 59.2 us  [per_device(): parts = [lax.ppermute(parts[0], 'seq', right), *parts]]
    all_gather x1 -> x0, waiting for transfers between devices: 49.7 us -> none  [per_device(): value_piece = lax.all_gather(values_own, 'seq', axis=0, tiled=True)]
    all_gather x1, waiting for transfers between devices: 37 us -> 8.4 us  [per_device(): key_piece = lax.all_gather(keys_own, 'seq', axis=0, tiled=True)]
    unnamed x18 -> x45, local copies, waits for them, and re-layouts: 0.43 us -> 9.6 us
  transfers between devices with their start and end apart: 8 -> 14, of which waited for: 7 -> 13; matrix products, arithmetic and copies ran while one was open for 8% -> 11% of each run, Pallas kernels for 0% -> 0%
where the time goes in v1:
time: 508 us; the launch traced here: 506 us
  waiting for transfers between devices  323 us (64%)
  matrix products  83.9 us (17%)
  other arithmetic  38.2 us (8%)
  local copies, waits for them, and re-layouts  34.6 us (7%)
  between operations  20.5 us (4%)
  starting transfers between devices  5.76 us (1%)
    all_gather x1, waiting for transfers between devices, per_device(): lax.all_gather(vit_qkv_w, 'seq', axis=0, tiled=True)  126 us
    ppermute x7, waiting for transfers between devices, per_device(): parts = [lax.ppermute(parts[0], 'seq', right), *parts]  59.2 us
    all_gather x1, waiting for transfers between devices, per_device(): lax.all_gather(vit_out_w, 'seq', axis=0, tiled=True)  44.6 us
    reduce_scatter x1, waiting for transfers between devices, per_device(): lax.psum_scatter(jnp.dot(context_tok, wo, preferred_element_type=jnp.floa...  43.3 us
    all_gather x1, waiting for transfers between devices, per_device(): shard_piece = lax.all_gather(normed_tok, 'frame', axis=0, tiled=True)  32.8 us
    dot_general x4, matrix products, visit(): jnp.einsum('qkgd,nkd->kgqn', grouped_rows, key_block, preferred_element_t...  23.4 us
    reduce_sum x4, other arithmetic, visit(): denominator = denominator * rescale + jnp.sum(expd, axis=-1)  18.6 us
    dot_general x4, matrix products, visit(): jnp.einsum('kgqn,nkd->kgqd', expd.astype(jnp.bfloat16), value_block, pref...  18.3 us
  transfers between devices with their start and end apart: 14, of which 13 were waited for; matrix products, arithmetic and copies ran while one was open for 11% of the time, Pallas kernels for 0%

profile of v1, /device:TPU:0, one launch (start us, length us, event | category | flops | bytes accessed | tf_op | source)
XLA Modules:
  0.0 506.3 jit_solution(15250584760435057879)
XLA Ops:
  28.3 126.2 %all-gather.5.cloned.1.call-done = bf16[1280,3840]{1,0:T(8,128)(2,1)} async-done(((bf16[160,3840]{1,0:T(8,128)(2,1)}), bf16[1280,3840]{1,0:T(8,128)(2,1)}) %all-gather.5.cloned.1.call-update) | async-done | bytes 9830416 | tf_op jit(solution)/shard_map/all_gather | solution.py:112
  154.5 7.9 %fusion.48 = bf16[256,3840]{1,0:T(8,128)(2,1)} fusion(bf16[1280,3840]{1,0:T(8,128)(2,1)} %all-gather.5.cloned.1.call-done, f32[3840]{0:T(1024)S(1)} %copy-done.11, bf16[1,256,1280]{2,1,0:T(8,128)(2,1)S(1)} %get-tuple-element.277, f32[1280]{0:T(1024)S(1)} %copy-done.12, f32[1280]{0:T(1024)S(1)} %copy-done.13, f32[256]{0:T(256)S(1)} %add_rsqrt_fusion, ...), kind=kOutput, calls=%fused_computation.75 | convolution fusion | flops 2520514560 | bytes 12479488 | tf_op jit(solution)/shard_map/dot_general | solution.py:43
  171.7 44.6 %all-gather.7.cloned.1.call-done = bf16[1280,1280]{1,0:T(8,128)(2,1)} async-done(((bf16[160,1280]{1,0:T(8,128)(2,1)}), bf16[1280,1280]{1,0:T(8,128)(2,1)}) %all-gather.7.cloned.1.call-update) | async-done | bytes 3276816 | tf_op jit(solution)/shard_map/all_gather | solution.py:128
  216.3 4.1 fusion.55
  230.3 7.7 %all-to-all-done = bf16[32,1,2,1280]{3,2,1,0:T(2,128)(2,1)S(1)} async-done(((bf16[32,1,2,1280]{3,2,1,0:T(2,128)(2,1)}), bf16[32,1,2,1280]{3,2,1,0:T(2,128)(2,1)S(1)}, u32[]{:S(2)}, u32[]{:S(2)}) %all-to-all-start) | async-done | bytes 163872 | tf_op jit(solution)/shard_map/all_to_all | solution.py:143
  239.0 6.3 %multiply_reduce_fusion = (f32[128]{0:T(128)S(1)}, f32[128,4096]{1,0:T(8,128)S(1)}) fusion(bf16[128,1,4096]{2,0,1:T(8,128)(2,1)} %param.24, f32[4096]{0:T(1024)S(1)} %copy-done.9, bf16[128,1280]{1,0:T(8,128)(2,1)S(1)} %gather_fusion.4, bf16[1280,4096]{1,0:T(8,128)(2,1)} %param.31, pred[128]{0:T(512)(128)(4,1)S(1)} %compare_and_fusion.1), kind=kOutput, calls=%fused_computation.93 | convolution fusion | flops 1345322880 | bytes 13976192 | tf_op jit(solution)/shard_map/dot_general | solution.py:153
  246.6 32.8 %all-gather.9.cloned.1.call-done = bf16[512,4096]{1,0:T(8,128)(2,1)} async-done(((bf16[128,4096]{1,0:T(8,128)(2,1)}), bf16[512,4096]{1,0:T(8,128)(2,1)}) %all-gather.9.cloned.1.call-update) | async-done | bytes 4194320 | tf_op jit(solution)/shard_map/all_gather | solution.py:164
  284.7 9.7 %collective-permute-done.1 = bf16[512,2,128]{2,0,1:T(8,128)(2,1)S(1)} collective-permute-done((bf16[512,2,128]{2,0,1:T(8,128)(2,1)S(1)}, bf16[512,2,128]{2,0,1:T(8,128)(2,1)S(1)}, u32[]{:S(2)}, u32[]{:S(2)}) %collective-permute-start.1) | collective-permute-done | bytes 262176 | tf_op jit(solution)/shard_map/ppermute | solution.py:208
  295.2 9.5 %collective-permute-done.2 = bf16[512,2,128]{2,0,1:T(8,128)(2,1)S(1)} collective-permute-done((bf16[512,2,128]{2,0,1:T(8,128)(2,1)S(1)}, bf16[512,2,128]{2,0,1:T(8,128)(2,1)S(1)}, u32[]{:S(2)}, u32[]{:S(2)}) %collective-permute-start.2) | collective-permute-done | bytes 262176 | tf_op jit(solution)/shard_map/ppermute | solution.py:208
  304.6 4.2 fusion.103
  309.3 4.7 collective-permute-done.3
  314.2 8.9 %collective-permute-done.4 = bf16[512,2,128]{2,0,1:T(8,128)(2,1)S(1)} collective-permute-done((bf16[512,2,128]{2,0,1:T(8,128)(2,1)S(1)}, bf16[512,2,128]{2,0,1:T(8,128)(2,1)S(1)}, u32[]{:S(2)}, u32[]{:S(2)}) %collective-permute-start.4) | collective-permute-done | bytes 262176 | tf_op jit(solution)/shard_map/ppermute | solution.py:208
  324.1 8.2 %collective-permute-done.5 = bf16[512,2,128]{2,0,1:T(8,128)(2,1)} collective-permute-done((bf16[512,2,128]{2,0,1:T(8,128)(2,1)S(1)}, bf16[512,2,128]{2,0,1:T(8,128)(2,1)}, u32[]{:S(2)}, u32[]{:S(2)}) %collective-permute-start.5) | collective-permute-done | bytes 262176 | tf_op jit(solution)/shard_map/ppermute | solution.py:208
  332.3 5.9 %fusion.104 = f32[512,512]{0,1:T(8,128)S(1)} fusion(bf16[512,4096]{1,0:T(8,128)(2,1)} %all-gather.9.cloned.1.call-done, bf16[4096,512]{1,0:T(8,128)(2,1)} %param.34), kind=kOutput, calls=%fused_computation.230 | convolution fusion | flops 2147483648 | bytes 9437184 | tf_op jit(solution)/shard_map/dot_general | solution.py:167
  338.3 10.6 %collective-permute-done.6 = bf16[512,2,128]{2,0,1:T(8,128)(2,1)} collective-permute-done((bf16[512,2,128]{2,0,1:T(8,128)(2,1)}, bf16[512,2,128]{2,0,1:T(8,128)(2,1)}, u32[]{:S(2)}, u32[]{:S(2)}) %collective-permute-start.6) | collective-permute-done | bytes 262176 | tf_op jit(solution)/shard_map/ppermute | solution.py:208
  350.7 7.6 %collective-permute-done.7 = bf16[512,2,128]{2,0,1:T(8,128)(2,1)} collective-permute-done((bf16[512,2,128]{2,0,1:T(8,128)(2,1)}, bf16[512,2,128]{2,0,1:T(8,128)(2,1)}, u32[]{:S(2)}, u32[]{:S(2)}) %collective-permute-start.7) | collective-permute-done | bytes 262176 | tf_op jit(solution)/shard_map/ppermute | solution.py:208
  369.1 8.4 %all-gather.11.cloned.1.call-done = bf16[4096,2,128]{2,0,1:T(8,128)(2,1)} async-done(((bf16[512,2,128]{2,0,1:T(8,128)(2,1)}), bf16[4096,2,128]{2,0,1:T(8,128)(2,1)}) %all-gather.11.cloned.1.call-update) | async-done | bytes 2097168 | tf_op jit(solution)/shard_map/all_gather | solution.py:203
  377.5 71.8 %while.20 = (s32[]{:T(128)}, f32[2,2,512]{2,1,0:T(2,128)S(1)}, f32[2,2,512]{2,1,0:T(2,128)S(1)}, f32[2,2,512,128]{3,2,1,0:T(8,128)S(1)}, s32[4]{0:T(128)S(1)}, /...) while((s32[]{:T(128)}, f32[2,2,512]{2,1,0:T(2,128)S(1)}, ...), condition=%wide.region_12.13_spmd.clone, body=%wide.region_9.12_spmd.clone.sunk | while | flops 1102377984 | bytes 64631976 | solution.py:243
  379.2 5.9 %fusion.134 = (f32[2,2,512]{2,1,0:T(2,128)S(1)}, f32[2,1024,512,2]{2,1,3,0:T(8,128)}) fusion(pred[512,1024]{0,1:T(8,128)(4,1)S(1)} %broadcast_compare_fusion.2, bf16[512,2,2,128]{3,0,2,1:T(8,128)(2,1)S(1)} %get-tuple-element.390, bf16[4,1024,2,128]{3,1,0,2:T(8,128)(2,1)} %get-tuple-element.389, s32[]{:T(128)} %get-tuple-element.373), kind=kOutput, calls=%fused_computation.8.clone.1 | convolution fusion | flops 543160320 | bytes 9970176 | tf_op jit(solution)/shard_map/while/body/eval_jaxpr/qkgd,nkd->kgqn/dot_general | solution.py:226
  385.0 4.6 fusion.136
  390.9 4.6 fusion.138
  397.1 5.9 %fusion.134 = (f32[2,2,512]{2,1,0:T(2,128)S(1)}, f32[2,1024,512,2]{2,1,3,0:T(8,128)}) fusion(pred[512,1024]{0,1:T(8,128)(4,1)S(1)} %broadcast_compare_fusion.2, bf16[512,2,2,128]{3,0,2,1:T(8,128)(2,1)S(1)} %get-tuple-element.390, bf16[4,1024,2,128]{3,1,0,2:T(8,128)(2,1)} %get-tuple-element.389, s32[]{:T(128)} %get-tuple-element.373), kind=kOutput, calls=%fused_computation.8.clone.1 | convolution fusion | flops 543160320 | bytes 9970176 | tf_op jit(solution)/shard_map/while/body/eval_jaxpr/qkgd,nkd->kgqn/dot_general | solution.py:226
  403.0 4.6 fusion.136
  408.8 4.6 fusion.138
  415.1 5.9 %fusion.134 = (f32[2,2,512]{2,1,0:T(2,128)S(1)}, f32[2,1024,512,2]{2,1,3,0:T(8,128)}) fusion(pred[512,1024]{0,1:T(8,128)(4,1)S(1)} %broadcast_compare_fusion.2, bf16[512,2,2,128]{3,0,2,1:T(8,128)(2,1)S(1)} %get-tuple-element.390, bf16[4,1024,2,128]{3,1,0,2:T(8,128)(2,1)} %get-tuple-element.389, s32[]{:T(128)} %get-tuple-element.373), kind=kOutput, calls=%fused_computation.8.clone.1 | convolution fusion | flops 543160320 | bytes 9970176 | tf_op jit(solution)/shard_map/while/body/eval_jaxpr/qkgd,nkd->kgqn/dot_general | solution.py:226
  421.0 4.6 fusion.136
  426.8 4.6 fusion.138
  433.0 5.9 %fusion.134 = (f32[2,2,512]{2,1,0:T(2,128)S(1)}, f32[2,1024,512,2]{2,1,3,0:T(8,128)}) fusion(pred[512,1024]{0,1:T(8,128)(4,1)S(1)} %broadcast_compare_fusion.2, bf16[512,2,2,128]{3,0,2,1:T(8,128)(2,1)S(1)} %get-tuple-element.390, bf16[4,1024,2,128]{3,1,0,2:T(8,128)(2,1)} %get-tuple-element.389, s32[]{:T(128)} %get-tuple-element.373), kind=kOutput, calls=%fused_computation.8.clone.1 | convolution fusion | flops 543160320 | bytes 9970176 | tf_op jit(solution)/shard_map/while/body/eval_jaxpr/qkgd,nkd->kgqn/dot_general | solution.py:226
  438.9 4.6 fusion.136
  444.7 4.6 fusion.138
  449.8 6.7 %convolution_convert_fusion = bf16[512,4096]{1,0:T(8,128)(2,1)} fusion(bf16[512,512]{0,1:T(8,128)(2,1)S(1)} %bitcast.138, bf16[512,4096]{1,0:T(8,128)(2,1)} %param.37), kind=kOutput, calls=%fused_computation.73 | convolution fusion | flops 2149580800 | bytes 8912896 | tf_op jit(solution)/shard_map/dot_general | solution.py:248
  456.5 43.3 %reduce-scatter.2.cloned.1.call-done = bf16[128,4096]{1,0:T(8,128)(2,1)} async-done(((bf16[512,4096]{1,0:T(8,128)(2,1)}), bf16[128,4096]{1,0:T(8,128)(2,1)}) %reduce-scatter.2.cloned.1.call-update) | async-done | bytes 1048592 | tf_op jit(solution)/shard_map/reduce_scatter | solution.py:247
  (167 shorter events, 68.0 us)
Async XLA Ops:
  6.5 272.9 %copy-start = (bf16[4096,256]{1,0:T(8,128)(2,1)S(1)}, bf16[4096,256]{1,0:T(8,128)(2,1)}, u32[]{:S(2)}) copy-start(bf16[4096,256]{1,0:T(8,128)(2,1)} %param.36) | copy-start | bytes 6291460
  6.5 147.9 %copy-start.13 = (f32[1280]{0:T(1024)S(1)}, f32[1280]{0:T(1024)}, u32[]{:S(2)}) copy-start(f32[1280]{0:T(1024)} %param.25) | copy-start | bytes 15364
  6.5 147.9 %copy-start.12 = (f32[1280]{0:T(1024)S(1)}, f32[1280]{0:T(1024)}, u32[]{:S(2)}) copy-start(f32[1280]{0:T(1024)} %param.26) | copy-start | bytes 15364
  6.5 148.0 %copy-start.11 = (f32[3840]{0:T(1024)S(1)}, f32[3840]{0:T(1024)}, u32[]{:S(2)}) copy-start(f32[3840]{0:T(1024)} %param.28) | copy-start | bytes 46084
  6.5 147.9 %all-gather.5.cloned.1.call-start = ((), (), s32[]{:S(2)}) async-start(), calls=%async_computation.2 | async-start | bytes 11059200 | tf_op jit(solution)/shard_map/all_gather | solution.py:112
  7.3 209.1 %all-gather.7.cloned.1.call-start = ((), (), s32[]{:S(2)}) async-start(), calls=%async_computation.3 | async-start | bytes 3686400 | tf_op jit(solution)/shard_map/all_gather | solution.py:128
  7.3 18.8 %collective-permute-start = (bf16[2,256,1280]{2,1,0:T(8,128)(2,1)}, bf16[2,256,1280]{2,1,0:T(8,128)(2,1)}, u32[]{:S(2)}, u32[]{:S(2)}) collective-permute-start(bf16[2,256,1280]{2,1,0:T(8,128)(2,1)} %param.20), channel_id=1, source_target_pairs={{0,8},{8,0},{16,24},{24,16},{1,9},{9,1},{17,25},{25,17},{2,10},{10... | collective-permute-start | bytes 3932168 | tf_op jit(solution)/shard_map/ppermute | solution.py:18
  170.1 46.2 %copy-start.14 = (f32[1280]{0:T(1024)S(1)}, f32[1280]{0:T(1024)}, u32[]{:S(2)}) copy-start(f32[1280]{0:T(1024)} %param.30) | copy-start | bytes 15364
  222.1 16.9 %copy-start.9 = (f32[4096]{0:T(1024)S(1)}, f32[4096]{0:T(1024)}, u32[]{:S(2)}) copy-start(f32[4096]{0:T(1024)} %param.32) | copy-start | bytes 49156
  226.7 11.3 %all-to-all-start = ((bf16[32,1,2,1280]{3,2,1,0:T(2,128)(2,1)}), bf16[32,1,2,1280]{3,2,1,0:T(2,128)(2,1)S(1)}, u32[]{:S(2)}, u32[]{:S(2)}) async-start(bf16[32,1,2,1280]{3,2,1,0:T(2,128)(2,1)} %broadcast_select_fusion.1), calls=%async_computation | async-start | bytes 327680 | tf_op jit(solution)/shard_map/all_to_all | solution.py:143
  230.0 49.4 %all-gather.9.cloned.1.call-start = ((), (), s32[]{:S(2)}) async-start(), calls=%async_computation.4 | async-start | bytes 5242880 | tf_op jit(solution)/shard_map/all_gather | solution.py:164
  239.0 6.3 %copy-start.10 = (f32[4096]{0:T(1024)S(1)}, f32[4096]{0:T(1024)}, u32[]{:S(2)}) copy-start(f32[4096]{0:T(1024)} %param.33) | copy-start | bytes 49156
  246.6 130.9 %all-gather.11.cloned.1.call-start = ((), (), s32[]{:S(2)}) async-start(), calls=%async_computation.5 | async-start | bytes 2359296 | tf_op jit(solution)/shard_map/all_gather | solution.py:203
  283.1 11.2 %collective-permute-start.1 = (bf16[512,2,128]{2,0,1:T(8,128)(2,1)S(1)}, bf16[512,2,128]{2,0,1:T(8,128)(2,1)S(1)}, u32[]{:S(2)}, u32[]{:S(2)}) collective-permute-start(bf16[512,2,128]{2,0,1:T(8,128)(2,1)S(1)} %copy.91), channel_id=1, source_target_pairs={{0,1},{1,2},{2,3},{3,4},{4,5},{5,6},{6,7},{7,0},{8,9},{9,10},{10,1... | collective-permute-start | bytes 786440 | tf_op jit(solution)/shard_map/ppermute | solution.py:208
  294.3 10.3 %collective-permute-start.2 = (bf16[512,2,128]{2,0,1:T(8,128)(2,1)S(1)}, bf16[512,2,128]{2,0,1:T(8,128)(2,1)S(1)}, u32[]{:S(2)}, u32[]{:S(2)}) collective-permute-start(bf16[512,2,128]{2,0,1:T(8,128)(2,1)S(1)} %collective-permute-done.1), channel_id=1, source_target_pairs={{0,1},{1,2},{2,3},{3,4},{4,5},{5,6},{6,7},{7,0},{8,9},{9,10},{10,1... | collective-permute-start | bytes 786440 | tf_op jit(solution)/shard_map/ppermute | solution.py:208
  304.6 4.3 copy-start.3
  304.6 9.4 %collective-permute-start.3 = (bf16[512,2,128]{2,0,1:T(8,128)(2,1)S(1)}, bf16[512,2,128]{2,0,1:T(8,128)(2,1)S(1)}, u32[]{:S(2)}, u32[]{:S(2)}) collective-permute-start(bf16[512,2,128]{2,0,1:T(8,128)(2,1)S(1)} %collective-permute-done.2), channel_id=1, source_target_pairs={{0,1},{1,2},{2,3},{3,4},{4,5},{5,6},{6,7},{7,0},{8,9},{9,10},{10,1... | collective-permute-start | bytes 786440 | tf_op jit(solution)/shard_map/ppermute | solution.py:208
  314.1 24.2 %copy-start.5 = (bf16[512,2,128]{2,0,1:T(8,128)(2,1)}, bf16[512,2,128]{2,0,1:T(8,128)(2,1)S(1)}, u32[]{:S(2)}) copy-start(bf16[512,2,128]{2,0,1:T(8,128)(2,1)S(1)} %collective-permute-done.3) | copy-start | bytes 786436
  314.1 9.1 %collective-permute-start.4 = (bf16[512,2,128]{2,0,1:T(8,128)(2,1)S(1)}, bf16[512,2,128]{2,0,1:T(8,128)(2,1)S(1)}, u32[]{:S(2)}, u32[]{:S(2)}) collective-permute-start(bf16[512,2,128]{2,0,1:T(8,128)(2,1)S(1)} %collective-permute-done.3), channel_id=1, source_target_pairs={{0,1},{1,2},{2,3},{3,4},{4,5},{5,6},{6,7},{7,0},{8,9},{9,10},{10,1... | collective-permute-start | bytes 786440 | tf_op jit(solution)/shard_map/ppermute | solution.py:208
  323.1 15.1 %copy-start.7 = (bf16[512,2,128]{2,0,1:T(8,128)(2,1)}, bf16[512,2,128]{2,0,1:T(8,128)(2,1)S(1)}, u32[]{:S(2)}) copy-start(bf16[512,2,128]{2,0,1:T(8,128)(2,1)S(1)} %collective-permute-done.4) | copy-start | bytes 786436
  323.1 9.2 %collective-permute-start.5 = (bf16[512,2,128]{2,0,1:T(8,128)(2,1)S(1)}, bf16[512,2,128]{2,0,1:T(8,128)(2,1)}, u32[]{:S(2)}, u32[]{:S(2)}) collective-permute-start(bf16[512,2,128]{2,0,1:T(8,128)(2,1)S(1)} %collective-permute-done.4), channel_id=1, source_target_pairs={{0,1},{1,2},{2,3},{3,4},{4,5},{5,6},{6,7},{7,0},{8,9},{9,10},{10,1... | collective-permute-start | bytes 786440 | tf_op jit(solution)/shard_map/ppermute | solution.py:208
  324.0 175.8 %reduce-scatter.2.cloned.1.call-start = ((), (), s32[]{:S(2)}) async-start(), calls=%async_computation.6 | async-start | bytes 5242880 | tf_op jit(solution)/shard_map/reduce_scatter | solution.py:247
  332.3 16.6 %collective-permute-start.6 = (bf16[512,2,128]{2,0,1:T(8,128)(2,1)}, bf16[512,2,128]{2,0,1:T(8,128)(2,1)}, u32[]{:S(2)}, u32[]{:S(2)}) collective-permute-start(bf16[512,2,128]{2,0,1:T(8,128)(2,1)} %collective-permute-done.5), channel_id=1, source_target_pairs={{0,1},{1,2},{2,3},{3,4},{4,5},{5,6},{6,7},{7,0},{8,9},{9,10},{10,1... | collective-permute-start | bytes 786440 | tf_op jit(solution)/shard_map/ppermute | solution.py:208
  348.9 9.5 %collective-permute-start.7 = (bf16[512,2,128]{2,0,1:T(8,128)(2,1)}, bf16[512,2,128]{2,0,1:T(8,128)(2,1)}, u32[]{:S(2)}, u32[]{:S(2)}) collective-permute-start(bf16[512,2,128]{2,0,1:T(8,128)(2,1)} %collective-permute-done.6), channel_id=1, source_target_pairs={{0,1},{1,2},{2,3},{3,4},{4,5},{5,6},{6,7},{7,0},{8,9},{9,10},{10,1... | collective-permute-start | bytes 786440 | tf_op jit(solution)/shard_map/ppermute | solution.py:208
  349.3 13.0 %copy-start.6 = (bf16[512,2,128]{2,0,1:T(8,128)(2,1)S(1)}, bf16[512,2,128]{2,0,1:T(8,128)(2,1)}, u32[]{:S(2)}) copy-start(bf16[512,2,128]{2,0,1:T(8,128)(2,1)} %copy-done.5) | copy-start | bytes 786436
  349.6 17.9 %copy-start.4 = (bf16[512,2,128]{2,0,1:T(8,128)(2,1)S(1)}, bf16[512,2,128]{2,0,1:T(8,128)(2,1)}, u32[]{:S(2)}) copy-start(bf16[512,2,128]{2,0,1:T(8,128)(2,1)} %copy-done.3) | copy-start | bytes 786436
  363.4 14.1 %copy-start.8 = (bf16[512,2,2,128]{3,0,2,1:T(8,128)(2,1)S(1)}, bf16[512,2,2,128]{3,0,2,1:T(8,128)(2,1)}, u32[]{:S(2)}) copy-start(bf16[512,2,2,128]{3,0,2,1:T(8,128)(2,1)} %pad_maximum_fusion) | copy-start | bytes 1572868
  385.0 5.8 %copy-start.2 = (f32[2,1024,512,2]{2,1,3,0:T(8,128)S(1)}, f32[2,1024,512,2]{2,1,3,0:T(8,128)}, u32[]{:S(2)}) copy-start(f32[2,1024,512,2]{2,1,3,0:T(8,128)} %get-tuple-element.359) | copy-start | bytes 25165828 | tf_op jit(solution)/shard_map/while
  403.0 5.8 %copy-start.2 = (f32[2,1024,512,2]{2,1,3,0:T(8,128)S(1)}, f32[2,1024,512,2]{2,1,3,0:T(8,128)}, u32[]{:S(2)}) copy-start(f32[2,1024,512,2]{2,1,3,0:T(8,128)} %get-tuple-element.359) | copy-start | bytes 25165828 | tf_op jit(solution)/shard_map/while
  420.9 5.8 %copy-start.2 = (f32[2,1024,512,2]{2,1,3,0:T(8,128)S(1)}, f32[2,1024,512,2]{2,1,3,0:T(8,128)}, u32[]{:S(2)}) copy-start(f32[2,1024,512,2]{2,1,3,0:T(8,128)} %get-tuple-element.359) | copy-start | bytes 25165828 | tf_op jit(solution)/shard_map/while
  438.9 5.8 %copy-start.2 = (f32[2,1024,512,2]{2,1,3,0:T(8,128)S(1)}, f32[2,1024,512,2]{2,1,3,0:T(8,128)}, u32[]{:S(2)}) copy-start(f32[2,1024,512,2]{2,1,3,0:T(8,128)} %get-tuple-element.359) | copy-start | bytes 25165828 | tf_op jit(solution)/shard_map/while
  449.8 50.0 %copy-start.1 = (bf16[4096,256]{1,0:T(8,128)(2,1)S(1)}, bf16[4096,256]{1,0:T(8,128)(2,1)}, u32[]{:S(2)}) copy-start(bf16[4096,256]{1,0:T(8,128)(2,1)} %param.36) | copy-start | bytes 6291460
Sparse Core Ops, SparseCore 0:
  9.5 144.9 all-gather.4
  156.7 59.6 all-gather.6
  246.7 32.7 all-gather.8
  324.1 53.3 all-gather.10
  456.6 43.1 reduce-scatter.1
